TPU v7x, 32 devices: a whole 2x2x4 slice. The times are simulated.
32 devices in a mesh: cols: 8 (over z, y), rows: 4 (over x, core).
Axes of the slice: x: 2, y: 2, z: 4, core: 2. Of those that a mesh axis runs over, the one named last changes fastest.
Arguments:
- gradient: bfloat16 [8192, 28672], P('rows', 'cols'), may hold values from -6 to 6
- eigenbasis: float32 [8192, 8192], P('rows', 'cols'), may hold values from -0.0625 to 0.0625
- first_moment: float32 [4, 256, 28672], P(None, 'rows', 'cols'), may hold values from -4 to 4
- second_moment: float32 [4, 256, 28672], P(None, 'rows', 'cols'), may hold values from 0.2 to 2
- prior_update: float32 [8192, 28672], P('rows', 'cols'), may hold values from -3 to 3
- group_ids: int32 [4], replicated, may hold values from 0 to 31, as said below
Outputs:
- first_out: float32 [4, 256, 28672], P(None, 'rows', 'cols')
- second_out: float32 [4, 256, 28672], P(None, 'rows', 'cols')
- update: float32 [8192, 28672], P('rows', 'cols')
Inputs may be any that keep to these rules, and one draw needn't show every extreme that they name: `group_ids`: the 4 entries are distinct.
All inputs are finite; a program needn't handle non-finite values.
Results may differ from a plain program's by a relative error of at most 0.0003.
Values sent between devices are 32-bit elements; how exact they have to be, the bound alone decides.
No kernel may reach another device: no remote copies, remote signals or barrier semaphores. Data moves between devices by JAX's collectives and lax.ppermute only.
A program may use at most 256 MiB of HBM per device.

v0:
```python
import jax
import jax.numpy as jnp
from jax import lax
from jax.sharding import PartitionSpec as P

GROUP = 256
GROUPS = 4
beta_one = 0.9
beta_two = 0.95
correct_one = 1.0 - 0.9**10
correct_two = 1.0 - 0.95**10
epsilon = 1e-08


def broadcast(block, axis, source):
    block = jnp.where(lax.axis_index(axis) == source, block, jnp.zeros_like(block))
    return lax.psum(block, axis)


def rotate_with(basis_part, grad_float):
    dims = (((0,), (0,)), ((), ()))
    return lax.dot_general(
        basis_part,
        grad_float,
        dims,
        precision=lax.Precision.HIGHEST,
        preferred_element_type=jnp.float32,
    )


def fetch_group(eigenbasis, group_index):
    width_dev = eigenbasis.shape[1]
    owners = max(1, GROUP // width_dev)
    span_cols = min(GROUP, width_dev)
    group_start = group_index * GROUP
    pieces = []
    for owner_slot in range(owners):
        piece_start = group_start + owner_slot * span_cols
        own_piece = lax.dynamic_slice_in_dim(eigenbasis, piece_start % width_dev, span_cols, 1)
        pieces.append(broadcast(own_piece, "cols", piece_start // width_dev))
    if owners > 1:
        return jnp.concatenate(pieces, axis=1)
    return pieces[0]


def per_device(gradient, eigenbasis, first_moment, second_moment, prior_update, group_ids):
    rows_here = first_moment.shape[1]
    grad_float = gradient.astype(jnp.float32)
    update = prior_update
    firsts = []
    seconds = []
    for group_slot in range(GROUPS):
        group_basis = fetch_group(eigenbasis, group_ids[group_slot])

        def rotate_rows(row_start, row_count, group_basis=group_basis):
            return rotate_with(group_basis, grad_float)

        rotated = lax.psum_scatter(
            rotate_rows(jnp.int32(0), rows_here * lax.axis_size("rows")),
            "rows",
            scatter_dimension=0,
            tiled=True,
        )
        moment_one = beta_one * first_moment[group_slot] + (1.0 - beta_one) * rotated
        moment_two = beta_two * second_moment[group_slot] + (1.0 - beta_two) * rotated * rotated
        adjusted = moment_one / correct_one / (jnp.sqrt(moment_two / correct_two) + epsilon)

        def add_back(total, piece, piece_row, group_basis=group_basis):
            return total + jnp.dot(
                group_basis,
                piece,
                precision=lax.Precision.HIGHEST,
                preferred_element_type=jnp.float32,
            )

        update = add_back(
            update, lax.all_gather(adjusted, "rows", axis=0, tiled=True), jnp.int32(0)
        )
        firsts.append(moment_one)
        seconds.append(moment_two)
    return (jnp.stack(firsts), jnp.stack(seconds), update)


def solution(mesh):
    placed = (
        P("rows", "cols"),
        P("rows", "cols"),
        P(None, "rows", "cols"),
        P(None, "rows", "cols"),
        P("rows", "cols"),
        P(),
    )
    return jax.shard_map(
        per_device,
        mesh=mesh,
        in_specs=placed,
        out_specs=(P(None, "rows", "cols"), P(None, "rows", "cols"), P("rows", "cols")),
        check_vma=False,
    )
```

profile of v0, /device:TPU:0, one launch (start us, length us, event | category | flops | bytes accessed | tf_op | source)
XLA Modules:
  0.0 680.0 jit_solution(14189288038641210160)
XLA Ops:
  7.2 0.0 all-reduce.3.cloned.1.call-start
  7.2 1.5 fusion.12
  11.4 9.7 %dynamic-slice_select_fusion.3 = (f32[2048,256]{1,0:T(8,128)}, f32[2048,256]{1,0:T(8,128)}, f32[2048,256]{1,0:T(8,128)}, f32[2048,256]{1,0:T(8,128)}) fusion(f32[2048,1024]{1,0:T(8,128)} %param.7, s32[]{:T(128)S(6)} %select_n.73, pred[]{:T(512)S(6)} %eq.17, s32[]{:T(128)S(6)} %select_n.78, pred[]{:T(512)S(6)} %eq.18, s32[]{:T(128)S(6)} %select_n.88, ...), kind=kLoop, calls=%fused_computation.6 | loop fusion | flops 2097152 | bytes 16777236 | tf_op jit(solution)/shard_map/jit(_where)/select_n | solution.py:16
  21.1 0.0 all-reduce.3.cloned.1.call-update
  21.1 0.0 reduce-scatter.11.cloned.1.call-start
  21.2 273.0 %all-reduce.3.cloned.1.call-done = (f32[2048,256]{1,0:T(8,128)}, f32[2048,256]{1,0:T(8,128)}, f32[2048,256]{1,0:T(8,128)}, f32[2048,256]{1,0:T(8,128)}) async-done(((f32[2048,256]{1,0:T(8,128)}, f32[2048,256]{1,0:T(8,128)}, f32[2048,256]{1,0:T(8,128)}, f32[2048,256]{1,0:T(8,128)}), (f32[2048,256]{1,0:T(8,128)}, f32[2048,256]{1,0:T(8,128)}, f32[2048,256]{1,0:T(8,128)}, ...) | async-done | bytes 8388624 | tf_op jit(solution)/shard_map/psum | solution.py:17
  294.1 17.1 %fusion.16 = f32[256,3584]{1,0:T(8,128)} fusion(f32[2048,256]{1,0:T(8,128)} %get-tuple-element.3, bf16[2048,3584]{1,0:T(8,128)(2,1)} %param.6), kind=kOutput, calls=%fused_computation.35 | convolution fusion | flops 22548578304 | bytes 20447232 | tf_op jit(solution)/shard_map/dot_general | solution.py:22
  311.2 0.0 copy-start.4
  311.3 0.0 reduce-scatter.11.cloned.1.call-update
  311.3 0.2 reduce-scatter.5.cloned.1.call-start
  311.5 1.3 copy-done.4
  312.8 16.6 %fusion.13 = f32[256,3584]{1,0:T(8,128)} fusion(f32[2048,256]{1,0:T(8,128)S(1)} %copy-done.4, bf16[2048,3584]{1,0:T(8,128)(2,1)} %param.6), kind=kOutput, calls=%fused_computation.32 | convolution fusion | flops 22548578304 | bytes 20447232 | tf_op jit(solution)/shard_map/dot_general | solution.py:22
  329.5 0.0 copy-start.2
  329.5 0.0 reduce-scatter.5.cloned.1.call-update
  329.5 0.3 reduce-scatter.7.cloned.1.call-start
  329.7 1.3 copy-done.2
  331.0 16.5 %fusion.14 = f32[256,3584]{1,0:T(8,128)} fusion(f32[2048,256]{1,0:T(8,128)S(1)} %copy-done.2, bf16[2048,3584]{1,0:T(8,128)(2,1)} %param.6), kind=kOutput, calls=%fused_computation.33 | convolution fusion | flops 22548578304 | bytes 20447232 | tf_op jit(solution)/shard_map/dot_general | solution.py:22
  347.6 0.0 copy-start.1
  347.6 0.0 reduce-scatter.7.cloned.1.call-update
  347.6 0.3 reduce-scatter.9.cloned.1.call-start
  347.9 1.3 copy-done.1
  349.2 16.6 %fusion.15 = f32[256,3584]{1,0:T(8,128)} fusion(f32[2048,256]{1,0:T(8,128)S(1)} %copy-done.1, bf16[2048,3584]{1,0:T(8,128)(2,1)} %param.6), kind=kOutput, calls=%fused_computation.34 | convolution fusion | flops 22548578304 | bytes 20447232 | tf_op jit(solution)/shard_map/dot_general | solution.py:22
  365.8 0.0 reduce-scatter.9.cloned.1.call-update
  365.8 0.0 all-gather.5.cloned.1.call-start
  365.8 0.0 reduce-scatter.11.cloned.1.call-done
  365.9 29.8 %reduce-scatter.5.cloned.1.call-done = f32[64,3584]{1,0:T(8,128)} async-done(((f32[256,3584]{1,0:T(8,128)}), f32[64,3584]{1,0:T(8,128)}) %reduce-scatter.5.cloned.1.call-update) | async-done | bytes 917520 | tf_op jit(solution)/shard_map/reduce_scatter | solution.py:58
  395.6 44.2 %reduce-scatter.7.cloned.1.call-done = f32[64,3584]{1,0:T(8,128)} async-done(((f32[256,3584]{1,0:T(8,128)}), f32[64,3584]{1,0:T(8,128)}) %reduce-scatter.7.cloned.1.call-update) | async-done | bytes 917520 | tf_op jit(solution)/shard_map/reduce_scatter | solution.py:58
  439.8 44.2 %reduce-scatter.9.cloned.1.call-done = f32[64,3584]{1,0:T(8,128)} async-done(((f32[256,3584]{1,0:T(8,128)}), f32[64,3584]{1,0:T(8,128)}) %reduce-scatter.9.cloned.1.call-update) | async-done | bytes 917520 | tf_op jit(solution)/shard_map/reduce_scatter | solution.py:58
  484.1 6.9 %add_divide_fusion = (f32[64,3584]{1,0:T(8,128)}, f32[64,3584]{1,0:T(8,128)}, f32[64,3584]{1,0:T(8,128)}, f32[64,3584]{1,0:T(8,128)}, f32[1,64,3584]{2,1,0:T(8,1...) fusion(f32[64,3584]{1,0:T(8,128)} %reduce-scatter.11.cloned.1.c, ...), kind=kLoop, calls=%fused_computation.19 | loop fusion | flops 10092544 | bytes 21102592 | tf_op jit(solution)/shard_map/div | solution.py:66
  491.0 0.0 all-gather.5.cloned.1.call-update
  491.0 0.0 all-gather.7.cloned.1.call-start
  491.1 0.7 all-gather.7.cloned.1.call-update
  491.8 0.0 all-gather.9.cloned.1.call-start
  491.8 0.7 all-gather.9.cloned.1.call-update
  492.5 0.5 all-gather.11.cloned.1.call-start
  493.0 0.2 all-gather.11.cloned.1.call-update
  493.3 1.6 fusion.7
  494.9 5.1 pad_maximum_fusion
  500.0 0.0 copy-start.3
  500.0 22.7 %all-gather.5.cloned.1.call-done = f32[256,3584]{1,0:T(8,128)} async-done(((f32[64,3584]{1,0:T(8,128)}), f32[256,3584]{1,0:T(8,128)}) %all-gather.5.cloned.1.call-update) | async-done | bytes 3670032 | tf_op jit(solution)/shard_map/all_gather | solution.py:77
  522.7 28.7 %fusion.17 = f32[2048,3584]{1,0:T(8,128)} fusion(f32[2048,256]{1,0:T(8,128)} %get-tuple-element.6, f32[256,3584]{1,0:T(8,128)} %all-gather.5.cloned.1.call-done), kind=kOutput, calls=%fused_computation.36 | convolution fusion | flops 22548578304 | bytes 35127296 | tf_op jit(solution)/shard_map/dot_general | solution.py:69
  551.4 4.4 all-gather.7.cloned.1.call-done
  555.7 0.0 copy-done.3
  555.7 28.4 %fusion.18 = f32[2048,3584]{1,0:T(8,128)} fusion(f32[2048,256]{1,0:T(8,128)S(1)} %copy-done.3, f32[256,3584]{1,0:T(8,128)} %all-gather.7.cloned.1.call-done), kind=kOutput, calls=%fused_computation.37 | convolution fusion | flops 22548578304 | bytes 35127296 | tf_op jit(solution)/shard_map/dot_general | solution.py:69
  584.1 0.0 copy-start
  584.1 5.3 all-gather.9.cloned.1.call-done
  589.4 28.9 %fusion.19 = f32[2048,3584]{1,0:T(8,128)} fusion(f32[2048,256]{1,0:T(8,128)} %get-tuple-element.4, f32[256,3584]{1,0:T(8,128)} %all-gather.9.cloned.1.call-done), kind=kOutput, calls=%fused_computation.38 | convolution fusion | flops 22548578304 | bytes 35127296 | tf_op jit(solution)/shard_map/dot_general | solution.py:69
  618.3 4.2 all-gather.11.cloned.1.call-done
  622.5 0.0 copy-done
  622.5 50.8 %add_add_fusion = f32[2048,3584]{1,0:T(8,128)} fusion(f32[2048,3584]{1,0:T(8,128)} %fusion.19, f32[2048,3584]{1,0:T(8,128)} %fusion.18, f32[2048,3584]{1,0:T(8,128)} %param.10, f32[2048,3584]{1,0:T(8,128)} %fusion.17, f32[2048,256]{1,0:T(8,128)S(1)} %copy-done, f32[256,3584]{1,0:T(8,128)} %all-gather.11.cloned.1.call-done), kind=kOutput, calls=%fused_computation | convolution fusion | flops 22577938432 | bytes 152567808 | tf_op jit(solution)/shard_map/dot_general | solution.py:69
Async XLA Ops:
  7.2 287.0 %all-reduce.3.cloned.1.call-start = ((), (), s32[]{:S(2)}) async-start(), calls=%async_computation.12 | async-start | bytes 16777216 | tf_op jit(solution)/shard_map/psum | solution.py:17
  21.1 344.7 %reduce-scatter.11.cloned.1.call-start = ((), (), s32[]{:S(2)}) async-start(), calls=%async_computation.7 | async-start | bytes 4587520 | tf_op jit(solution)/shard_map/reduce_scatter | solution.py:58
  311.2 1.6 copy-start.4
  311.3 84.3 %reduce-scatter.5.cloned.1.call-start = ((), (), s32[]{:S(2)}) async-start(), calls=%async_computation.4 | async-start | bytes 4587520 | tf_op jit(solution)/shard_map/reduce_scatter | solution.py:58
  329.5 1.6 copy-start.2
  329.5 110.4 %reduce-scatter.7.cloned.1.call-start = ((), (), s32[]{:S(2)}) async-start(), calls=%async_computation.5 | async-start | bytes 4587520 | tf_op jit(solution)/shard_map/reduce_scatter | solution.py:58
  347.6 1.6 copy-start.1
  347.6 136.5 %reduce-scatter.9.cloned.1.call-start = ((), (), s32[]{:S(2)}) async-start(), calls=%async_computation.6 | async-start | bytes 4587520 | tf_op jit(solution)/shard_map/reduce_scatter | solution.py:58
  365.8 156.9 %all-gather.5.cloned.1.call-start = ((), (), s32[]{:S(2)}) async-start(), calls=%async_computation.8 | async-start | bytes 4587520 | tf_op jit(solution)/shard_map/all_gather | solution.py:77
  491.0 64.7 %all-gather.7.cloned.1.call-start = ((), (), s32[]{:S(2)}) async-start(), calls=%async_computation.9 | async-start | bytes 4587520 | tf_op jit(solution)/shard_map/all_gather | solution.py:77
  491.8 97.6 %all-gather.9.cloned.1.call-start = ((), (), s32[]{:S(2)}) async-start(), calls=%async_computation.10 | async-start | bytes 4587520 | tf_op jit(solution)/shard_map/all_gather | solution.py:77
  492.5 129.9 %all-gather.11.cloned.1.call-start = ((), (), s32[]{:S(2)}) async-start(), calls=%async_computation.11 | async-start | bytes 4587520 | tf_op jit(solution)/shard_map/all_gather | solution.py:77
  500.0 55.7 %copy-start.3 = (f32[2048,256]{1,0:T(8,128)S(1)}, f32[2048,256]{1,0:T(8,128)}, u32[]{:S(2)}) copy-start(f32[2048,256]{1,0:T(8,128)} %get-tuple-element.5) | copy-start | bytes 6291460
  584.1 38.4 %copy-start = (f32[2048,256]{1,0:T(8,128)S(1)}, f32[2048,256]{1,0:T(8,128)}, u32[]{:S(2)}) copy-start(f32[2048,256]{1,0:T(8,128)} %get-tuple-element.3) | copy-start | bytes 6291460
Sparse Core Ops, SparseCore 0:
  21.2 272.8 all-reduce.2
  311.4 40.3 reduce-scatter.10
  354.3 41.2 reduce-scatter.4
  398.6 41.2 reduce-scatter.6
  442.8 41.2 reduce-scatter.8
  491.1 31.4 all-gather.4
  524.2 31.4 all-gather.6
  557.9 31.4 all-gather.8
  590.9 31.4 all-gather.10
where the time goes:
time: 687 us; the launch traced here: 680 us
  waiting for transfers between devices  429 us (62%)
  matrix products  204 us (30%)
  other arithmetic  23.4 us (3%)
  between operations  16.8 us (2%)
    psum x1, waiting for transfers between devices, broadcast(): return lax.psum(block, axis)  273 us
    dot_general x4, matrix products, add_back(): jnp.dot(group_basis, piece, precision=lax.Precision.HIGHEST, preferred_el...  137 us
    reduce_scatter x4, waiting for transfers between devices, per_device(): lax.psum_scatter(rotate_rows(jnp.int32(0), rows_here * lax.axis_size('row...  118 us
    dot_general x4, matrix products, rotate_with(): lax.dot_general(basis_part, grad_float, dims, precision=lax.Precision.HIG...  66.8 us
    all_gather x4, waiting for transfers between devices, per_device(): lax.all_gather(adjusted, 'rows', axis=0, tiled=True)  36.5 us
  transfers between devices with their start and end apart: 9, of which 8 were waited for; matrix products, arithmetic and copies ran while one was open for 21% of the time, Pallas kernels for 0%

commit v1 on v0

--- a/solution.py
+++ b/solution.py
@@ -14,7 +14,7 @@
 
 def broadcast(block, axis, source):
     block = jnp.where(lax.axis_index(axis) == source, block, jnp.zeros_like(block))
-    return lax.psum(block, axis)
+    return jnp.sum(lax.all_gather(block, axis), axis=0)
 
 
 def rotate_with(basis_part, grad_float):

time: 687 us -> 1310 us (1.91)
  waiting for transfers between devices: 429 us -> 1020 us
  other arithmetic: 23.4 us -> 56.5 us
    all_gather x0 -> x4, waiting for transfers between devices: none -> 832 us  [broadcast(): return jnp.sum(lax.all_gather(block, axis), axis=0)]
    psum x1 -> x0, waiting for transfers between devices: 273 us -> none  [broadcast(): return lax.psum(block, axis)]
    reduce_sum x0 -> x4, other arithmetic: none -> 32.5 us  [broadcast(): return jnp.sum(lax.all_gather(block, axis), axis=0)]
    reduce_scatter x4, waiting for transfers between devices: 118 us -> 148 us  [per_device(): lax.psum_scatter(rotate_rows(jnp.int32(0), rows_here * lax.axis_size('row...]
  transfers between devices with their start and end apart: 9 -> 12, of which waited for: 8 -> 12; matrix products, arithmetic and copies ran while one was open for 21% -> 15% of each run, Pallas kernels for 0% -> 0%
where the time goes in v1:
time: 1310 us
  waiting for transfers between devices  1020 us (78%)
  matrix products  210 us (16%)
  other arithmetic  56.5 us (4%)
  between operations  17.4 us (1%)
    all_gather x4, waiting for transfers between devices, broadcast(): return jnp.sum(lax.all_gather(block, axis), axis=0)  832 us
    reduce_scatter x4, waiting for transfers between devices, per_device(): lax.psum_scatter(rotate_rows(jnp.int32(0), rows_here * lax.axis_size('row...  148 us
    dot_general x4, matrix products, add_back(): jnp.dot(group_basis, piece, precision=lax.Precision.HIGHEST, preferred_el...  137 us
    dot_general x4, matrix products, rotate_with(): lax.dot_general(basis_part, grad_float, dims, precision=lax.Precision.HIG...  72.7 us
    all_gather x4, waiting for transfers between devices, per_device(): lax.all_gather(adjusted, 'rows', axis=0, tiled=True)  35.8 us
    reduce_sum x4, other arithmetic, broadcast(): return jnp.sum(lax.all_gather(block, axis), axis=0)  32.5 us
  transfers between devices with their start and end apart: 12, of which 12 were waited for; matrix products, arithmetic and copies ran while one was open for 15% of the time, Pallas kernels for 0%

profile of v1, /device:TPU:0, one launch (start us, length us, event | category | flops | bytes accessed | tf_op | source)
XLA Modules:
  0.0 1306.3 jit_solution(441750178527648244)
XLA Ops:
  7.2 0.0 all-gather.27.cloned.1.call-start
  7.2 1.4 fusion.12
  11.3 9.7 dynamic-slice_select_fusion.3
  21.1 0.0 all-gather.27.cloned.1.call-update
  21.1 0.0 all-gather.21.cloned.1.call-start
  21.1 0.7 all-gather.21.cloned.1.call-update
  21.8 0.0 all-gather.23.cloned.1.call-start
  21.9 0.7 all-gather.23.cloned.1.call-update
  22.6 0.0 all-gather.25.cloned.1.call-start
  22.6 0.5 all-gather.25.cloned.1.call-update
  23.2 0.0 reduce-scatter.11.cloned.1.call-start
  23.2 228.1 %all-gather.27.cloned.1.call-done = f32[16384,256]{1,0:T(8,128)} async-done(((f32[2048,256]{1,0:T(8,128)}), f32[16384,256]{1,0:T(8,128)}) %all-gather.27.cloned.1.call-update) | async-done | bytes 16777232 | tf_op jit(solution)/shard_map/all_gather | solution.py:17
  251.3 7.1 reduce_sum.39
  258.4 17.7 %fusion.16 = f32[256,3584]{1,0:T(8,128)} fusion(f32[2048,256]{1,0:T(8,128)S(1)} %reduce_sum.39, bf16[2048,3584]{1,0:T(8,128)(2,1)} %param.6), kind=kOutput, calls=%fused_computation.35 | convolution fusion | flops 22548578304 | bytes 20447232 | tf_op jit(solution)/shard_map/dot_general | solution.py:22
  276.1 0.0 reduce-scatter.11.cloned.1.call-update
  276.2 0.3 reduce-scatter.5.cloned.1.call-start
  276.4 203.0 %all-gather.21.cloned.1.call-done = f32[16384,256]{1,0:T(8,128)} async-done(((f32[2048,256]{1,0:T(8,128)}), f32[16384,256]{1,0:T(8,128)}) %all-gather.21.cloned.1.call-update) | async-done | bytes 16777232 | tf_op jit(solution)/shard_map/all_gather | solution.py:17
  479.4 8.4 reduce_sum.36
  487.9 18.5 %fusion.13 = f32[256,3584]{1,0:T(8,128)} fusion(f32[2048,256]{1,0:T(8,128)} %reduce_sum.36, bf16[2048,3584]{1,0:T(8,128)(2,1)} %param.6), kind=kOutput, calls=%fused_computation.32 | convolution fusion | flops 22548578304 | bytes 20447232 | tf_op jit(solution)/shard_map/dot_general | solution.py:22
  506.4 0.0 reduce-scatter.5.cloned.1.call-update
  506.4 0.4 reduce-scatter.7.cloned.1.call-start
  506.9 200.8 %all-gather.23.cloned.1.call-done = f32[16384,256]{1,0:T(8,128)} async-done(((f32[2048,256]{1,0:T(8,128)}), f32[16384,256]{1,0:T(8,128)}) %all-gather.23.cloned.1.call-update) | async-done | bytes 16777232 | tf_op jit(solution)/shard_map/all_gather | solution.py:17
  707.6 8.5 reduce_sum.37
  716.1 18.4 %fusion.14 = f32[256,3584]{1,0:T(8,128)} fusion(f32[2048,256]{1,0:T(8,128)} %reduce_sum.37, bf16[2048,3584]{1,0:T(8,128)(2,1)} %param.6), kind=kOutput, calls=%fused_computation.33 | convolution fusion | flops 22548578304 | bytes 20447232 | tf_op jit(solution)/shard_map/dot_general | solution.py:22
  734.5 0.0 reduce-scatter.7.cloned.1.call-update
  734.5 0.2 reduce-scatter.9.cloned.1.call-start
  734.7 200.4 %all-gather.25.cloned.1.call-done = f32[16384,256]{1,0:T(8,128)} async-done(((f32[2048,256]{1,0:T(8,128)}), f32[16384,256]{1,0:T(8,128)}) %all-gather.25.cloned.1.call-update) | async-done | bytes 16777232 | tf_op jit(solution)/shard_map/all_gather | solution.py:17
  935.1 8.5 reduce_sum.38
  943.6 18.1 %fusion.15 = f32[256,3584]{1,0:T(8,128)} fusion(f32[2048,256]{1,0:T(8,128)} %reduce_sum.38, bf16[2048,3584]{1,0:T(8,128)(2,1)} %param.6), kind=kOutput, calls=%fused_computation.34 | convolution fusion | flops 22548578304 | bytes 20447232 | tf_op jit(solution)/shard_map/dot_general | solution.py:22
  961.7 0.0 reduce-scatter.9.cloned.1.call-update
  961.7 0.0 all-gather.13.cloned.1.call-start
  961.8 15.8 %reduce-scatter.11.cloned.1.call-done = f32[64,3584]{1,0:T(8,128)} async-done(((f32[256,3584]{1,0:T(8,128)}), f32[64,3584]{1,0:T(8,128)}) %reduce-scatter.11.cloned.1.call-update) | async-done | bytes 917520 | tf_op jit(solution)/shard_map/reduce_scatter | solution.py:58
  977.5 43.6 %reduce-scatter.5.cloned.1.call-done = f32[64,3584]{1,0:T(8,128)} async-done(((f32[256,3584]{1,0:T(8,128)}), f32[64,3584]{1,0:T(8,128)}) %reduce-scatter.5.cloned.1.call-update) | async-done | bytes 917520 | tf_op jit(solution)/shard_map/reduce_scatter | solution.py:58
  1021.2 44.4 %reduce-scatter.7.cloned.1.call-done = f32[64,3584]{1,0:T(8,128)} async-done(((f32[256,3584]{1,0:T(8,128)}), f32[64,3584]{1,0:T(8,128)}) %reduce-scatter.7.cloned.1.call-update) | async-done | bytes 917520 | tf_op jit(solution)/shard_map/reduce_scatter | solution.py:58
  1065.5 44.4 %reduce-scatter.9.cloned.1.call-done = f32[64,3584]{1,0:T(8,128)} async-done(((f32[256,3584]{1,0:T(8,128)}), f32[64,3584]{1,0:T(8,128)}) %reduce-scatter.9.cloned.1.call-update) | async-done | bytes 917520 | tf_op jit(solution)/shard_map/reduce_scatter | solution.py:58
  1109.9 7.2 add_divide_fusion
  1117.1 0.0 all-gather.13.cloned.1.call-update
  1117.1 0.0 all-gather.15.cloned.1.call-start
  1117.1 0.5 all-gather.15.cloned.1.call-update
  1117.7 0.0 all-gather.17.cloned.1.call-start
  1117.7 0.7 all-gather.17.cloned.1.call-update
  1118.4 0.3 all-gather.19.cloned.1.call-start
  1118.7 0.3 all-gather.19.cloned.1.call-update
  1119.0 1.6 fusion.7
  1120.6 5.4 pad_maximum_fusion
  1126.0 22.7 %all-gather.13.cloned.1.call-done = f32[256,3584]{1,0:T(8,128)} async-done(((f32[64,3584]{1,0:T(8,128)}), f32[256,3584]{1,0:T(8,128)}) %all-gather.13.cloned.1.call-update) | async-done | bytes 3670032 | tf_op jit(solution)/shard_map/all_gather | solution.py:77
  1148.7 28.7 %fusion.17 = f32[2048,3584]{1,0:T(8,128)} fusion(f32[2048,256]{1,0:T(8,128)} %reduce_sum.36, f32[256,3584]{1,0:T(8,128)} %all-gather.13.cloned.1.call-done), kind=kOutput, calls=%fused_computation.36 | convolution fusion | flops 22548578304 | bytes 35127296 | tf_op jit(solution)/shard_map/dot_general | solution.py:69
  1177.4 4.2 all-gather.15.cloned.1.call-done
  1181.6 28.7 %fusion.18 = f32[2048,3584]{1,0:T(8,128)} fusion(f32[2048,256]{1,0:T(8,128)} %reduce_sum.37, f32[256,3584]{1,0:T(8,128)} %all-gather.15.cloned.1.call-done), kind=kOutput, calls=%fused_computation.37 | convolution fusion | flops 22548578304 | bytes 35127296 | tf_op jit(solution)/shard_map/dot_general | solution.py:69
  1210.3 4.9 all-gather.17.cloned.1.call-done
  1215.3 29.0 %fusion.19 = f32[2048,3584]{1,0:T(8,128)} fusion(f32[2048,256]{1,0:T(8,128)} %reduce_sum.38, f32[256,3584]{1,0:T(8,128)} %all-gather.17.cloned.1.call-done), kind=kOutput, calls=%fused_computation.38 | convolution fusion | flops 22548578304 | bytes 35127296 | tf_op jit(solution)/shard_map/dot_general | solution.py:69
  1244.3 4.0 all-gather.19.cloned.1.call-done
  1248.2 50.8 %add_add_fusion = f32[2048,3584]{1,0:T(8,128)} fusion(f32[2048,3584]{1,0:T(8,128)} %fusion.19, f32[2048,3584]{1,0:T(8,128)} %fusion.18, f32[2048,3584]{1,0:T(8,128)} %param.10, f32[2048,3584]{1,0:T(8,128)} %fusion.17, f32[2048,256]{1,0:T(8,128)S(1)} %reduce_sum.39, f32[256,3584]{1,0:T(8,128)} %all-gather.19.cloned.1.call-done), kind=kOutput, calls=%fused_computation | convolution fusion | flops 22577938432 | bytes 152567808 | tf_op jit(solution)/shard_map/dot_general | solution.py:69
Async XLA Ops:
  7.2 244.1 %all-gather.27.cloned.1.call-start = ((), (), s32[]{:S(2)}) async-start(), calls=%async_computation.15 | async-start | bytes 18874368 | tf_op jit(solution)/shard_map/all_gather | solution.py:17
  21.1 458.4 %all-gather.21.cloned.1.call-start = ((), (), s32[]{:S(2)}) async-start(), calls=%async_computation.12 | async-start | bytes 18874368 | tf_op jit(solution)/shard_map/all_gather | solution.py:17
  21.8 685.8 %all-gather.23.cloned.1.call-start = ((), (), s32[]{:S(2)}) async-start(), calls=%async_computation.13 | async-start | bytes 18874368 | tf_op jit(solution)/shard_map/all_gather | solution.py:17
  22.6 912.5 %all-gather.25.cloned.1.call-start = ((), (), s32[]{:S(2)}) async-start(), calls=%async_computation.14 | async-start | bytes 18874368 | tf_op jit(solution)/shard_map/all_gather | solution.py:17
  23.2 954.4 %reduce-scatter.11.cloned.1.call-start = ((), (), s32[]{:S(2)}) async-start(), calls=%async_computation.7 | async-start | bytes 4587520 | tf_op jit(solution)/shard_map/reduce_scatter | solution.py:58
  276.2 745.0 %reduce-scatter.5.cloned.1.call-start = ((), (), s32[]{:S(2)}) async-start(), calls=%async_computation.4 | async-start | bytes 4587520 | tf_op jit(solution)/shard_map/reduce_scatter | solution.py:58
  506.4 559.1 %reduce-scatter.7.cloned.1.call-start = ((), (), s32[]{:S(2)}) async-start(), calls=%async_computation.5 | async-start | bytes 4587520 | tf_op jit(solution)/shard_map/reduce_scatter | solution.py:58
  734.5 375.4 %reduce-scatter.9.cloned.1.call-start = ((), (), s32[]{:S(2)}) async-start(), calls=%async_computation.6 | async-start | bytes 4587520 | tf_op jit(solution)/shard_map/reduce_scatter | solution.py:58
  961.7 187.0 %all-gather.13.cloned.1.call-start = ((), (), s32[]{:S(2)}) async-start(), calls=%async_computation.8 | async-start | bytes 4587520 | tf_op jit(solution)/shard_map/all_gather | solution.py:77
  1117.1 64.5 %all-gather.15.cloned.1.call-start = ((), (), s32[]{:S(2)}) async-start(), calls=%async_computation.9 | async-start | bytes 4587520 | tf_op jit(solution)/shard_map/all_gather | solution.py:77
  1117.7 97.6 %all-gather.17.cloned.1.call-start = ((), (), s32[]{:S(2)}) async-start(), calls=%async_computation.10 | async-start | bytes 4587520 | tf_op jit(solution)/shard_map/all_gather | solution.py:77
  1118.4 129.8 %all-gather.19.cloned.1.call-start = ((), (), s32[]{:S(2)}) async-start(), calls=%async_computation.11 | async-start | bytes 4587520 | tf_op jit(solution)/shard_map/all_gather | solution.py:77
Sparse Core Ops, SparseCore 0:
  21.2 229.9 all-gather.26
  253.9 225.4 all-gather.20
  482.1 225.4 all-gather.22
  709.6 225.4 all-gather.24
  938.1 39.4 reduce-scatter.10
  979.9 41.2 reduce-scatter.4
  1024.3 41.2 reduce-scatter.6
  1068.6 41.2 reduce-scatter.8
  1117.2 31.4 all-gather.12
  1150.1 31.4 all-gather.14
  1183.8 31.4 all-gather.16
  1216.7 31.4 all-gather.18
